TPU v7x, 128 devices: a whole 4x4x4 slice. The times are simulated.
128 devices in a mesh: section: 2 (over x_hi), grp: 64 (over y, z, x_lo, core).
Axes of the slice: x: 4 (x_hi: 2, x_lo: 2; x = x_hi * 2 + x_lo), y: 4, z: 4, core: 2. Of those that a mesh axis runs over, the one named last changes fastest.
Arguments:
- voltages: bfloat16 [1024, 524288], P('grp', 'section'), may hold values from -6 to 6
- filter_taps: float32 [8, 512], replicated, may hold values from -2 to 2
- beam_weights: bfloat16 [256, 2, 512, 1024], P('grp'), may hold values from -0.125 to 0.125
- antenna_of_row: int32 [1024], replicated, may hold values from 0 to 1023, each once
- beam_delay: int32 [512], P('grp'), may hold values from 0 to 127
Outputs:
- dedispersed: float32 [256, 2, 512, 1024], P(None, None, 'grp', 'section')
Inputs may be any that keep to these rules, and one draw needn't show every extreme that they name: A permutation: voltage row r holds physical antenna antenna_of_row[r].
All inputs are finite; a program needn't handle non-finite values.
Results may differ from a plain program's by a relative error of at most 0.0069.
Values may be sent and summed in bfloat16 or wider, within the bound.
A program may use at most 128 MiB of HBM per device.

v0:
```python
import math
import jax
import jax.numpy as jnp
from jax import lax
from jax.sharding import PartitionSpec as P

DFT_LEN = 256


def shifted(value, axis, steps):
    count = lax.axis_size(axis)
    leading, last = (max(0, -steps), min(count, count - steps))
    return lax.ppermute(value, axis, [(source, source + steps) for source in range(leading, last)])


def dft_table(frame_length, group_count, split_ways):
    channels = frame_length // 2
    per_target = channels // (group_count * split_ways)
    column = jnp.arange(frame_length, dtype=jnp.int32)
    target = column // (2 * per_target)
    within = column % (2 * per_target)
    quadrature = within // per_target
    channel = (
        target % group_count * (per_target * split_ways)
        + target // group_count * per_target
        + within % per_target
    )
    sample = jnp.arange(frame_length, dtype=jnp.int32)[:, None]
    winding = sample * channel[None, :] % frame_length
    angles = 2.0 * math.pi / frame_length * winding.astype(jnp.float32)
    factor = channels ** (-0.5)
    dft_cols = jnp.where(
        quadrature[None, :] == 0, jnp.cos(angles) * factor, -jnp.sin(angles) * factor
    )
    return dft_cols.astype(jnp.bfloat16)


def block_tables(length):
    half_len = length // 2
    factor = length ** (-0.5)
    sample = jnp.arange(length, dtype=jnp.int32)
    angles = (
        2.0 * math.pi / length * (sample[:, None] * sample[None, :] % length).astype(jnp.float32)
    )
    cosine_table = (jnp.cos(angles) * factor).astype(jnp.bfloat16)
    sine_table = (jnp.sin(angles) * factor).astype(jnp.bfloat16)
    forward_real = jnp.concatenate([cosine_table, -sine_table], axis=1)
    forward_imag = jnp.concatenate([sine_table, cosine_table], axis=1)
    back_cos = cosine_table[:, half_len:]
    back_sin = sine_table[:, half_len:]
    inverse_real = jnp.concatenate([back_cos, back_sin], axis=1)
    inverse_imag = jnp.concatenate([-back_sin, back_cos], axis=1)
    return (forward_real, forward_imag, inverse_real, inverse_imag)


def chirp_factor(delays, channel_count, channels, length):
    frequency = jnp.arange(length, dtype=jnp.int32)
    signed = jnp.where(frequency < length // 2, frequency, frequency - length).astype(jnp.float32)
    channel = jnp.arange(channel_count, dtype=jnp.int32).astype(jnp.float32)
    strength = (1.0 + channel / channels) ** (-3.0)
    sweep = signed * signed / (length * length)
    phases = (math.pi * delays.astype(jnp.float32))[None, :, None] * strength[
        :, None, None
    ] * sweep[None, None, :] - 0.5 * math.pi * frequency.astype(jnp.float32)[None, None, :]
    return (jnp.cos(phases), jnp.sin(phases))


def dedisperse(series, leading, delays, tables, channels):
    forward_real, forward_imag, inverse_real, inverse_imag = tables
    length = forward_real.shape[0]
    advance = length // 2
    chan_count = series.shape[0]
    beam_count = series.shape[2]
    time_len = series.shape[3]
    block_count = time_len // advance
    joined = jnp.concatenate([leading, series], axis=3).reshape(
        chan_count, 2, beam_count, block_count + 1, advance
    )
    blocks = jnp.concatenate([joined[:, :, :, :-1, :], joined[:, :, :, 1:, :]], axis=4)
    spectrum = jnp.einsum(
        "cbml,lk->cbmk", blocks[:, 0], forward_real, preferred_element_type=jnp.float32
    ) + jnp.einsum("cbml,lk->cbmk", blocks[:, 1], forward_imag, preferred_element_type=jnp.float32)
    chirp_real, chirp_imag = chirp_factor(delays, chan_count, channels, length)
    chirp_real = chirp_real[:, :, None, :]
    chirp_imag = chirp_imag[:, :, None, :]
    spec_real = spectrum[..., :length]
    spec_imag = spectrum[..., length:]
    filtered_real = (spec_real * chirp_real - spec_imag * chirp_imag).astype(jnp.bfloat16)
    filtered_imag = (spec_real * chirp_imag + spec_imag * chirp_real).astype(jnp.bfloat16)
    result = jnp.einsum(
        "cbmk,kn->cbmn", filtered_real, inverse_real, preferred_element_type=jnp.float32
    ) + jnp.einsum("cbmk,kn->cbmn", filtered_imag, inverse_imag, preferred_element_type=jnp.float32)
    out_real = result[..., :advance].reshape(chan_count, beam_count, time_len)
    out_imag = result[..., advance:].reshape(chan_count, beam_count, time_len)
    return jnp.stack([out_real, out_imag], axis=1)


def local(voltages, filter_taps, beam_weights, antenna_of_row, beam_delay):
    group_count = lax.axis_size("grp")
    antenna_row_set = voltages.shape[0]
    samples = voltages.shape[1]
    filter_tap_count = filter_taps.shape[0]
    frame_length = filter_taps.shape[1]
    channel_spectra = samples // frame_length
    channels = frame_length // 2
    antennas = antenna_of_row.shape[0]
    beam_count = beam_weights.shape[2]
    past_samples = shifted(
        voltages[:, samples - (filter_tap_count - 1) * frame_length :], "section", 1
    )
    extended = jnp.concatenate([past_samples, voltages], axis=1).reshape(
        antenna_row_set, channel_spectra + filter_tap_count - 1, frame_length
    )
    weighted = filter_taps[0] * extended[:, 0:channel_spectra, :]
    for tap_index in range(1, filter_tap_count):
        weighted = (
            weighted
            + filter_taps[tap_index] * extended[:, tap_index : tap_index + channel_spectra, :]
        )
    weighted = weighted.astype(jnp.bfloat16)
    split_ways = 1
    dft_cols = dft_table(frame_length, group_count, split_ways)
    channelised = jnp.einsum(
        "asp,pj->ajs", weighted, dft_cols, preferred_element_type=jnp.float32
    ).astype(jnp.bfloat16)[None]
    per_target = channels // (group_count * split_ways)
    ordered = jnp.take(beam_weights, antenna_of_row, axis=3).reshape(
        per_target, 2 * beam_count, antennas
    )
    tables = block_tables(DFT_LEN)
    received = lax.all_to_all(channelised, "grp", split_axis=2, concat_axis=0, tiled=True)
    item_count = received.shape[3]
    halves = received.shape[0] * received.shape[1] // antennas
    all_rows = received.reshape(halves, antennas, 2 * per_target, item_count)
    with_real = jnp.einsum(
        "cba,hacs->cbhs",
        ordered,
        all_rows[:, :, :per_target, :],
        preferred_element_type=jnp.float32,
    )
    with_imag = jnp.einsum(
        "cba,hacs->cbhs",
        ordered,
        all_rows[:, :, per_target:, :],
        preferred_element_type=jnp.float32,
    )
    beam_real = with_real[:, :beam_count] - with_imag[:, beam_count:]
    beam_imag = with_imag[:, :beam_count] + with_real[:, beam_count:]
    formed = jnp.stack([beam_real, beam_imag], axis=1).astype(jnp.bfloat16)
    arrival_buffer = lax.all_to_all(
        formed.reshape(per_target, 2, beam_count, channel_spectra),
        "grp",
        split_axis=2,
        concat_axis=0,
        tiled=True,
    )
    leading = shifted(arrival_buffer[:, :, :, channel_spectra - DFT_LEN // 2 :], "section", 1)
    result = dedisperse(arrival_buffer, leading, beam_delay, tables, channels)
    return result


def solution(mesh):
    in_specs = (P("grp", "section"), P(), P("grp", None, None, None), P(), P("grp"))
    out_specs = P(None, None, "grp", "section")
    return jax.shard_map(local, mesh=mesh, in_specs=in_specs, out_specs=out_specs, check_vma=False)
```

profile of v0, /device:TPU:70, one launch (start us, length us, event | category | flops | bytes accessed | tf_op | source)
XLA Modules:
  0.0 427.6 jit_solution(12808330259375173368)
XLA Ops:
  0.0 0.9 slice.107
  0.9 1.3 collective-permute-start
  2.2 5.1 %fusion.86 = bf16[512,512,1]{0,1,2:T(8,128)(2,1)S(1)} fusion(s32[512]{0:T(512)S(1)} %fusion.57, pred[512]{0:T(512)(128)(4,1)S(1)} %fusion.50), kind=kLoop, calls=%fused_computation.50.clone.clone.2 | loop fusion | flops 4980736 | bytes 526848 | tf_op jit(solution)/shard_map/asp,pj->ajs/dot_general | solution.py:123
  7.3 1.0 fusion.80
  8.3 0.9 collective-permute-done
  9.2 7.2 %pad_maximum_fusion = bf16[16,265728]{1,0:T(8,128)(2,1)} fusion(bf16[16,262144]{1,0:T(8,128)(2,1)} %param.5, bf16[16,3584]{1,0:T(8,128)(2,1)S(1)} %collective-permute-done), kind=kLoop, calls=%fused_computation.3 | loop fusion | flops 17006592 | bytes 17006592 | tf_op jit(solution)/shard_map/concatenate | solution.py:111
  16.4 12.4 %reshape.188 = bf16[16,519,512]{2,1,0:T(8,128)(2,1)} reshape(bf16[16,265728]{1,0:T(8,128)(2,1)} %pad_maximum_fusion) | data formatting | bytes 17006592 | tf_op jit(solution)/shard_map/reshape | solution.py:111
  28.7 44.7 %convert_bitcast_fusion = bf16[1,16,512,512]{3,2,1,0:T(8,128)(2,1)} fusion(bf16[16,519,512]{2,1,0:T(8,128)(2,1)} %reshape.188, f32[512]{0:T(512)S(1)} %bitcast.97, f32[512]{0:T(512)S(1)} %bitcast.98, f32[512]{0:T(512)S(1)} %bitcast.92, f32[512]{0:T(512)S(1)} %bitcast.93, f32[512]{0:T(512)S(1)} %bitcast.94, f32[512]{0:T(512)S(1)} %bitcast.95, ...), kind=kOutput, calls=%fused_computation.8 | convolution fusion | flops 4399824896 | bytes 76038144 | tf_op jit(solution)/shard_map/asp,pj->ajs/dot_general | solution.py:123
  73.4 11.4 %copy.43 = bf16[1,16,512,512]{3,1,0,2:T(8,128)(2,1)} copy(bf16[1,16,512,512]{3,2,1,0:T(8,128)(2,1)} %convert_bitcast_fusion) | data formatting | bytes 16777216 | tf_op jit(solution)/shard_map/broadcast_in_dim | solution.py:123
  84.8 9.8 %all-to-all-start = ((bf16[1,16,512,512]{3,1,0,2:T(8,128)(2,1)}), bf16[1,16,512,512]{3,1,0,2:T(8,128)(2,1)}, u32[]{:S(2)}, u32[]{:S(2)}) async-start(bf16[1,16,512,512]{3,1,0,2:T(8,128)(2,1)} %copy.43), calls=%async_computation | async-start | bytes 16777216 | tf_op jit(solution)/shard_map/all_to_all | solution.py:131
  94.6 0.0 copy-start
  94.6 14.8 %copy.41 = bf16[4,2,512,1024]{2,0,3,1:T(4,128)(2,1)} copy(bf16[4,2,512,1024]{3,2,1,0:T(8,128)(2,1)} %param.7) | data formatting | bytes 16777216 | tf_op args[2]
  109.4 0.0 copy-done
  109.4 19.0 %gather_fusion = bf16[1024,4,2,512]{3,1,2,0:T(4,128)(2,1)} fusion(bf16[4,2,512,1024]{2,0,3,1:T(4,128)(2,1)} %copy.41, s32[1024]{0:T(1024)S(1)} %fusion.49), kind=kCustom, calls=%fused_computation | custom fusion | bytes 16781312 | tf_op jit(solution)/shard_map/jit(_take)/gather | solution.py:127
  128.4 13.7 %copy.42 = bf16[4,2,512,1024]{3,2,1,0:T(8,128)(2,1)} copy(bf16[4,2,512,1024]{2,0,1,3:T(4,128)(2,1)} %bitcast.81) | data formatting | bytes 16777216 | tf_op jit(solution)/shard_map/jit(_take)/gather | solution.py:127
  142.1 7.3 %bitcast_select_fusion = bf16[4,1024,1024]{2,1,0:T(8,128)(2,1)} fusion(bf16[4,2,512,1024]{3,2,1,0:T(8,128)(2,1)} %copy.42, pred[1024]{0:T(1024)(128)(4,1)S(1)} %compare_and_fusion), kind=kLoop, calls=%fused_computation.5 | loop fusion | flops 4194304 | bytes 16778240 | tf_op jit(solution)/shard_map/jit(_take)/select_n | solution.py:127
  149.4 62.7 %all-to-all-done = bf16[1,16,512,512]{3,1,0,2:T(8,128)(2,1)} async-done(((bf16[1,16,512,512]{3,1,0,2:T(8,128)(2,1)}), bf16[1,16,512,512]{3,1,0,2:T(8,128)(2,1)}, u32[]{:S(2)}, u32[]{:S(2)}) %all-to-all-start) | async-done | bytes 8388640 | tf_op jit(solution)/shard_map/all_to_all | solution.py:131
  212.1 0.0 slice-start
  212.1 8.3 %copy.44 = bf16[1,16,64,8,512]{4,1,2,3,0:T(8,128)(2,1)} copy(bf16[1,16,64,8,512]{4,1,3,2,0:T(8,128)(2,1)} %bitcast.13) | data formatting | bytes 16777216 | tf_op jit(solution)/shard_map/all_to_all | solution.py:131
  220.5 0.0 slice-start.1
  220.5 8.3 %fusion.12 = f32[4,1024,1,512]{3,1,0,2:T(8,128)S(1)} fusion(bf16[4,1024,1024]{2,1,0:T(8,128)(2,1)} %bitcast_select_fusion, bf16[1,1024,8,512]{3,1,2,0:T(8,128)(2,1)} %bitcast.89), kind=kOutput, calls=%fused_computation.32 | convolution fusion | flops 4294967296 | bytes 20971520 | tf_op jit(solution)/shard_map/cba,hacs->cbhs/dot_general | solution.py:135
  228.8 0.0 slice-done
  228.8 0.0 slice-done.1
  228.8 9.0 %fusion.13 = f32[4,1024,1,512]{3,1,0,2:T(8,128)} fusion(bf16[4,1024,1024]{2,1,0:T(8,128)(2,1)S(1)} %bitcast.88, bf16[1,1024,8,512]{3,1,2,0:T(8,128)(2,1)} %bitcast.90), kind=kOutput, calls=%fused_computation.33 | convolution fusion | flops 4294967296 | bytes 20971520 | tf_op jit(solution)/shard_map/cba,hacs->cbhs/dot_general | solution.py:141
  237.8 4.3 fusion.15
  242.0 0.4 pad_maximum_fusion.2
  242.4 5.2 %copy.45 = bf16[4,2,512,512]{3,0,1,2:T(4,128)(2,1)} copy(bf16[4,2,512,512]{3,2,0,1:T(8,128)(2,1)S(1)} %pad_maximum_fusion.2) | data formatting | bytes 8388608 | tf_op jit(solution)/shard_map/stack | solution.py:149
  247.7 9.0 %all-to-all-start.1 = ((bf16[4,2,512,512]{3,0,1,2:T(4,128)(2,1)}), bf16[4,2,512,512]{3,0,1,2:T(4,128)(2,1)}, u32[]{:S(2)}, u32[]{:S(2)}) async-start(bf16[4,2,512,512]{3,0,1,2:T(4,128)(2,1)} %copy.45), calls=%async_computation.1 | async-start | bytes 8388608 | tf_op jit(solution)/shard_map/all_to_all | solution.py:150
  256.7 1.0 fusion.48
  257.7 1.1 multiply_convert_fusion
  258.8 0.0 copy-start.1
  258.8 52.8 %all-to-all-done.1 = bf16[4,2,512,512]{3,0,1,2:T(4,128)(2,1)} async-done(((bf16[4,2,512,512]{3,0,1,2:T(4,128)(2,1)}), bf16[4,2,512,512]{3,0,1,2:T(4,128)(2,1)}, u32[]{:S(2)}, u32[]{:S(2)}) %all-to-all-start.1) | async-done | bytes 4194336 | tf_op jit(solution)/shard_map/all_to_all | solution.py:150
  311.7 3.6 copy.65
  315.2 0.5 copy.47
  315.8 0.3 slice.156
  316.0 1.3 collective-permute-start.1
  317.4 0.0 copy-done.1
  317.4 0.1 broadcast_multiply_fusion
  317.5 7.4 %fusion.18 = (f32[256,8,256]{2,0,1:T(8,128)S(1)}, f32[256,8,256]{2,0,1:T(8,128)S(1)}) fusion(f32[256]{0:T(256)S(1)} %get-tuple-element.26, f32[256]{0:T(256)S(1)} %get-tuple-element.25, f32[256,8]{0,1:T(8,128)S(1)} %broadcast_multiply_fusion), kind=kLoop, calls=%fused_computation.39 | loop fusion | flops 1048576 | bytes 4204544 | tf_op jit(solution)/shard_map/cos | solution.py:65
  324.9 19.2 %collective-permute-done.1 = bf16[256,2,8,128]{3,2,1,0:T(8,128)(2,1)S(1)} collective-permute-done((bf16[256,2,8,128]{3,2,1,0:T(8,128)(2,1)S(1)}, bf16[256,2,8,128]{3,2,1,0:T(8,128)(2,1)S(1)}, u32[]{:S(2)}, u32[]{:S(2)}) %collective-permute-start.1) | collective-permute-done | bytes 1048608 | tf_op jit(solution)/shard_map/ppermute | solution.py:13
  344.0 1.1 maximum_bitcast_fusion
  345.2 2.6 fusion.79
  347.8 2.7 copy_dynamic-update-slice_fusion.1
  350.5 3.4 copy_dynamic-update-slice_fusion
  353.9 8.1 %fusion.3 = f32[256,8,4,512]{3,0,2,1:T(8,128)} fusion(bf16[256,2,8,4,256]{4,0,3,2,1:T(8,128)(2,1)S(1)} %copy_dynamic-update-slice_fusion, bf16[256,256]{1,0:T(8,128)(2,1)S(1)} %fusion.48, bf16[256,256]{1,0:T(8,128)(2,1)S(1)} %get-tuple-element.24), kind=kOutput, calls=%fused_computation.15 | convolution fusion | flops 2148007936 | bytes 21233664 | tf_op jit(solution)/shard_map/cbml,lk->cbmk/dot_general | solution.py:80
  362.0 13.9 %convolution_add_fusion = f32[256,8,4,512]{3,0,2,1:T(8,128)} fusion(f32[256,8,4,512]{3,0,2,1:T(8,128)} %fusion.3, bf16[256,2,8,4,256]{4,0,3,2,1:T(8,128)(2,1)S(1)} %copy_dynamic-update-slice_fusion, bf16[256,256]{1,0:T(8,128)(2,1)S(1)} %get-tuple-element.24, bf16[256,256]{1,0:T(8,128)(2,1)S(1)} %get-tuple-element.23), kind=kOutput, calls=%fused_computation.2 | convolution fusion | flops 2152202240 | bytes 38010880 | tf_op jit(solution)/shard_map/cbml,lk->cbmk/dot_general | solution.py:82
  375.9 10.9 %fusion.1 = f32[256,8,4,256]{0,3,2,1:T(8,128)} fusion(f32[256,8,4,512]{3,0,2,1:T(8,128)} %convolution_add_fusion, f32[256,8,256]{2,0,1:T(8,128)S(1)} %get-tuple-element.22, f32[256,8,256]{2,0,1:T(8,128)S(1)} %get-tuple-element.21, bf16[256,128]{1,0:T(8,128)(2,1)S(1)} %get-tuple-element.12, bf16[256,128]{1,0:T(8,128)(2,1)S(1)} %slice.163), kind=kOutput, calls=%fused_computation.11 | convolution fusion | flops 1082392576 | bytes 29491200 | tf_op jit(solution)/shard_map/cbmk,kn->cbmn/dot_general | solution.py:90
  386.8 13.5 %fusion.14 = f32[256,8,4,256]{0,3,2,1:T(8,128)} fusion(f32[256,8,4,256]{0,3,2,1:T(8,128)} %fusion.1, f32[256,8,4,512]{3,0,2,1:T(8,128)} %convolution_add_fusion, f32[256,8,256]{2,0,1:T(8,128)S(1)} %get-tuple-element.22, f32[256,8,256]{2,0,1:T(8,128)S(1)} %get-tuple-element.21, bf16[256,128]{1,0:T(8,128)(2,1)S(1)} %slice.163, ...), kind=kOutput, calls=%fused_computation.34 | convolution fusion | flops 1084489728 | bytes 37879808 | tf_op jit(solution)/shard_map/cbmk,kn->cbmn/dot_general | solution.py:92
  400.2 7.7 %fusion.78 = (f32[256,8,4,128]{0,3,2,1:T(8,128)}, f32[256,8,4,128]{0,3,2,1:T(8,128)}) fusion(f32[256,8,4,256]{0,3,2,1:T(8,128)} %fusion.14), kind=kLoop, calls=%fused_computation.136 | loop fusion | bytes 16777216 | tf_op jit(solution)/shard_map/slice | solution.py:93
  407.9 5.6 %copy.52 = f32[256,1,8,512]{3,2,1,0:T(8,128)} copy(f32[256,1,8,512]{0,3,2,1:T(8,128)} %bitcast.86) | data formatting | bytes 8388608 | tf_op jit(solution)/shard_map/stack;reshape | solution.py:95
  413.6 5.5 %copy.53 = f32[256,1,8,512]{3,2,1,0:T(8,128)} copy(f32[256,1,8,512]{0,3,2,1:T(8,128)} %bitcast.85) | data formatting | bytes 8388608 | tf_op jit(solution)/shard_map/stack;reshape | solution.py:95
  419.1 8.1 %pad_maximum_fusion.1 = f32[256,2,8,512]{3,2,1,0:T(8,128)} fusion(f32[256,1,8,512]{3,2,1,0:T(8,128)} %copy.53, f32[256,1,8,512]{3,2,1,0:T(8,128)} %copy.52), kind=kLoop, calls=%fused_computation.4 | loop fusion | flops 2097152 | bytes 16777216 | tf_op jit(solution)/shard_map/stack | solution.py:95
  (10 shorter events, 0.1 us)
Async XLA Ops:
  0.9 8.3 %collective-permute-start = (bf16[16,3584]{1,0:T(8,128)(2,1)S(1)}, bf16[16,3584]{1,0:T(8,128)(2,1)S(1)}, u32[]{:S(2)}, u32[]{:S(2)}) collective-permute-start(bf16[16,3584]{1,0:T(8,128)(2,1)S(1)} %slice.107), channel_id=1, source_target_pairs={{0,64},{1,65},{2,66},{3,67},{4,68},{5,69},{6,70},{7,71},{8,72},{9,... | collective-permute-start | bytes 344072 | tf_op jit(solution)/shard_map/ppermute | solution.py:13
  84.8 127.4 %all-to-all-start = ((bf16[1,16,512,512]{3,1,0,2:T(8,128)(2,1)}), bf16[1,16,512,512]{3,1,0,2:T(8,128)(2,1)}, u32[]{:S(2)}, u32[]{:S(2)}) async-start(bf16[1,16,512,512]{3,1,0,2:T(8,128)(2,1)} %copy.43), calls=%async_computation | async-start | bytes 16777216 | tf_op jit(solution)/shard_map/all_to_all | solution.py:131
  94.6 14.8 %copy-start = (s32[1024]{0:T(1024)S(1)}, s32[1024]{0:T(1024)}, u32[]{:S(2)}) copy-start(s32[1024]{0:T(1024)} %param.8) | copy-start | bytes 12292
  212.1 16.6 %slice-start = ((s8[8388608]{0:T(1024)(128)(4,1)}), s8[4194304]{0:T(1024)(128)(4,1)S(1)}, s32[]{:S(2)}) async-start(s8[8388608]{0:T(1024)(128)(4,1)} %bitcast.87), calls=%async_computation.2 | async-start | bytes 8388608
  220.5 8.3 %slice-start.1 = ((s8[8388608]{0:T(1024)(128)(4,1)}), s8[4194304]{0:T(1024)(128)(4,1)S(1)}, s32[]{:S(2)}) async-start(s8[8388608]{0:T(1024)(128)(4,1)} %bitcast.87), calls=%async_computation.3 | async-start | bytes 8388608
  247.7 64.0 %all-to-all-start.1 = ((bf16[4,2,512,512]{3,0,1,2:T(4,128)(2,1)}), bf16[4,2,512,512]{3,0,1,2:T(4,128)(2,1)}, u32[]{:S(2)}, u32[]{:S(2)}) async-start(bf16[4,2,512,512]{3,0,1,2:T(4,128)(2,1)} %copy.45), calls=%async_computation.1 | async-start | bytes 8388608 | tf_op jit(solution)/shard_map/all_to_all | solution.py:150
  258.8 58.5 %copy-start.1 = (s32[8]{0:T(128)S(1)}, s32[8]{0:T(128)}, u32[]{:S(2)}) copy-start(s32[8]{0:T(128)} %param.9) | copy-start | bytes 100
  316.0 28.0 %collective-permute-start.1 = (bf16[256,2,8,128]{3,2,1,0:T(8,128)(2,1)S(1)}, bf16[256,2,8,128]{3,2,1,0:T(8,128)(2,1)S(1)}, u32[]{:S(2)}, u32[]{:S(2)}) collective-permute-start(bf16[256,2,8,128]{3,2,1,0:T(8,128)(2,1)S(1)} %slice.156), channel_id=1, source_target_pairs={{0,64},{1,65},{2,66},{3,67},{4,68},{5,69},{6,70},{7,71},{8,72},{9,... | collective-permute-start | bytes 3145736 | tf_op jit(solution)/shard_map/ppermute | solution.py:13
where the time goes:
time: 436 us; the launch traced here: 428 us
  waiting for transfers between devices  136 us (31%)
  local copies, waits for them, and re-layouts  119 us (27%)
  matrix products  108 us (25%)
  other arithmetic  43.1 us (10%)
  starting transfers between devices  21.4 us (5%)
    all_to_all x1, waiting for transfers between devices, local(): lax.all_to_all(channelised, 'grp', split_axis=2, concat_axis=0, tiled=True)  62.7 us
    all_to_all x1, waiting for transfers between devices, local(): lax.all_to_all(formed.reshape(per_target, 2, beam_count, channel_spectra)...  52.8 us
    dot_general x1, matrix products, local(): jnp.einsum('asp,pj->ajs', weighted, dft_cols, preferred_element_type=jnp....  44.7 us
    gather x2, local copies, waits for them, and re-layouts, local(): jnp.take(beam_weights, antenna_of_row, axis=3)  32.6 us
    ppermute x2, waiting for transfers between devices, shifted(): lax.ppermute(value, axis, [(source, source + steps) for source in range(l...  20 us
    unnamed x10, local copies, waits for them, and re-layouts  17.5 us
    dot_general x1, matrix products, dedisperse(): jnp.einsum('cbml,lk->cbmk', blocks[:, 1], forward_imag, preferred_element...  13.9 us
    dot_general x1, matrix products, dedisperse(): jnp.einsum('cbmk,kn->cbmn', filtered_imag, inverse_imag, preferred_elemen...  13.5 us
  transfers between devices with their start and end apart: 4, of which 4 were waited for; matrix products, arithmetic and copies ran while one was open for 16% of the time, Pallas kernels for 0%

commit v1 on v0

--- a/solution.py
+++ b/solution.py
@@ -147,13 +147,12 @@
     beam_real = with_real[:, :beam_count] - with_imag[:, beam_count:]
     beam_imag = with_imag[:, :beam_count] + with_real[:, beam_count:]
     formed = jnp.stack([beam_real, beam_imag], axis=1).astype(jnp.bfloat16)
-    arrival_buffer = lax.all_to_all(
-        formed.reshape(per_target, 2, beam_count, channel_spectra),
-        "grp",
-        split_axis=2,
-        concat_axis=0,
-        tiled=True,
-    )
+    w_in = formed.reshape(per_target, 2, beam_count, channel_spectra)
+    big = lax.axis_size("grp")
+    met_up = jnp.split(w_in, big, 2)
+    high = jnp.stack(met_up, 0)
+    now = lax.all_to_all(high, concat_axis=0, axis_name="grp", split_axis=0)
+    arrival_buffer = jnp.concatenate(now, 0)
     leading = shifted(arrival_buffer[:, :, :, channel_spectra - DFT_LEN // 2 :], "section", 1)
     result = dedisperse(arrival_buffer, leading, beam_delay, tables, channels)
     return result

time: 436 us -> 470 us (1.078)
  other arithmetic: 43.1 us -> 83.3 us
  local copies, waits for them, and re-layouts: 119 us -> 112 us
    unnamed x1 -> x64, other arithmetic: 0.01 us -> 39.9 us
    another operation x1 -> x0, local copies, waits for them, and re-layouts: 5.25 us -> none  [local(): formed = jnp.stack([beam_real, beam_imag], axis=1).astype(jnp.bfloat16)]
  transfers between devices with their start and end apart: 4 -> 4, of which waited for: 4 -> 4; matrix products, arithmetic and copies ran while one was open for 16% -> 15% of each run, Pallas kernels for 0% -> 0%
where the time goes in v1:
time: 470 us; the launch traced here: 461 us
  waiting for transfers between devices  135 us (29%)
  local copies, waits for them, and re-layouts  112 us (24%)
  matrix products  108 us (23%)
  other arithmetic  83.3 us (18%)
  starting transfers between devices  21.6 us (5%)
    all_to_all x1, waiting for transfers between devices, local(): lax.all_to_all(channelised, 'grp', split_axis=2, concat_axis=0, tiled=True)  62.7 us
    all_to_all x1, waiting for transfers between devices, local(): now = lax.all_to_all(high, concat_axis=0, axis_name='grp', split_axis=0)  52.8 us
    dot_general x1, matrix products, local(): jnp.einsum('asp,pj->ajs', weighted, dft_cols, preferred_element_type=jnp....  44.7 us
    unnamed x64, other arithmetic  39.9 us
    gather x2, local copies, waits for them, and re-layouts, local(): jnp.take(beam_weights, antenna_of_row, axis=3)  32.6 us
    ppermute x2, waiting for transfers between devices, shifted(): lax.ppermute(value, axis, [(source, source + steps) for source in range(l...  19.8 us
    unnamed x10, local copies, waits for them, and re-layouts  17.5 us
    dot_general x1, matrix products, dedisperse(): jnp.einsum('cbml,lk->cbmk', blocks[:, 1], forward_imag, preferred_element...  13.9 us
  transfers between devices with their start and end apart: 4, of which 4 were waited for; matrix products, arithmetic and copies ran while one was open for 15% of the time, Pallas kernels for 0%

profile of v1, /device:TPU:70, one launch (start us, length us, event | category | flops | bytes accessed | tf_op | source)
XLA Modules:
  0.0 461.2 jit_solution(2829862141855970004)
XLA Ops:
  0.0 0.9 slice.107
  0.9 1.3 collective-permute-start
  2.2 5.1 %fusion.150 = bf16[512,512,1]{0,1,2:T(8,128)(2,1)S(1)} fusion(s32[512]{0:T(512)S(1)} %fusion.121, pred[512]{0:T(512)(128)(4,1)S(1)} %fusion.114), kind=kLoop, calls=%fused_computation.174.clone.clone.2 | loop fusion | flops 4980736 | bytes 526848 | tf_op jit(solution)/shard_map/asp,pj->ajs/dot_general | solution.py:123
  7.3 1.0 fusion.144
  8.3 0.9 collective-permute-done
  9.2 7.2 %pad_maximum_fusion = bf16[16,265728]{1,0:T(8,128)(2,1)} fusion(bf16[16,262144]{1,0:T(8,128)(2,1)} %param.5, bf16[16,3584]{1,0:T(8,128)(2,1)S(1)} %collective-permute-done), kind=kLoop, calls=%fused_computation.129 | loop fusion | flops 17006592 | bytes 17006592 | tf_op jit(solution)/shard_map/concatenate | solution.py:111
  16.4 12.4 %reshape.191 = bf16[16,519,512]{2,1,0:T(8,128)(2,1)} reshape(bf16[16,265728]{1,0:T(8,128)(2,1)} %pad_maximum_fusion) | data formatting | bytes 17006592 | tf_op jit(solution)/shard_map/reshape | solution.py:111
  28.7 44.7 %convert_bitcast_fusion = bf16[1,16,512,512]{3,2,1,0:T(8,128)(2,1)} fusion(bf16[16,519,512]{2,1,0:T(8,128)(2,1)} %reshape.191, f32[512]{0:T(512)S(1)} %bitcast.221, f32[512]{0:T(512)S(1)} %bitcast.222, f32[512]{0:T(512)S(1)} %bitcast.216, f32[512]{0:T(512)S(1)} %bitcast.217, f32[512]{0:T(512)S(1)} %bitcast.218, f32[512]{0:T(512)S(1)} %bitcast.219, ...), kind=kOutput, calls=%fused_computation.134 | convolution fusion | flops 4399824896 | bytes 76038144 | tf_op jit(solution)/shard_map/asp,pj->ajs/dot_general | solution.py:123
  73.4 11.4 %copy.32 = bf16[1,16,512,512]{3,1,0,2:T(8,128)(2,1)} copy(bf16[1,16,512,512]{3,2,1,0:T(8,128)(2,1)} %convert_bitcast_fusion) | data formatting | bytes 16777216 | tf_op jit(solution)/shard_map/broadcast_in_dim | solution.py:123
  84.8 9.8 %all-to-all-start = ((bf16[1,16,512,512]{3,1,0,2:T(8,128)(2,1)}), bf16[1,16,512,512]{3,1,0,2:T(8,128)(2,1)}, u32[]{:S(2)}, u32[]{:S(2)}) async-start(bf16[1,16,512,512]{3,1,0,2:T(8,128)(2,1)} %copy.32), calls=%async_computation | async-start | bytes 16777216 | tf_op jit(solution)/shard_map/all_to_all | solution.py:131
  94.6 14.8 %copy.30 = bf16[4,2,512,1024]{2,0,3,1:T(4,128)(2,1)} copy(bf16[4,2,512,1024]{3,2,1,0:T(8,128)(2,1)} %param.7) | data formatting | bytes 16777216 | tf_op args[2]
  109.4 19.0 %gather_fusion = bf16[1024,4,2,512]{3,1,2,0:T(4,128)(2,1)} fusion(bf16[4,2,512,1024]{2,0,3,1:T(4,128)(2,1)} %copy.30, s32[1024]{0:T(1024)S(1)} %fusion.113), kind=kCustom, calls=%fused_computation | custom fusion | bytes 16781312 | tf_op jit(solution)/shard_map/jit(_take)/gather | solution.py:127
  128.4 13.7 %copy.31 = bf16[4,2,512,1024]{3,2,1,0:T(8,128)(2,1)} copy(bf16[4,2,512,1024]{2,0,1,3:T(4,128)(2,1)} %bitcast.206) | data formatting | bytes 16777216 | tf_op jit(solution)/shard_map/jit(_take)/gather | solution.py:127
  142.1 7.3 %bitcast_select_fusion = bf16[4,1024,1024]{2,1,0:T(8,128)(2,1)} fusion(bf16[4,2,512,1024]{3,2,1,0:T(8,128)(2,1)} %copy.31, pred[1024]{0:T(1024)(128)(4,1)S(1)} %compare_and_fusion), kind=kLoop, calls=%fused_computation.131 | loop fusion | flops 4194304 | bytes 16778240 | tf_op jit(solution)/shard_map/jit(_take)/select_n | solution.py:127
  149.4 62.7 %all-to-all-done = bf16[1,16,512,512]{3,1,0,2:T(8,128)(2,1)} async-done(((bf16[1,16,512,512]{3,1,0,2:T(8,128)(2,1)}), bf16[1,16,512,512]{3,1,0,2:T(8,128)(2,1)}, u32[]{:S(2)}, u32[]{:S(2)}) %all-to-all-start) | async-done | bytes 8388640 | tf_op jit(solution)/shard_map/all_to_all | solution.py:131
  212.1 8.3 %copy.33 = bf16[1,16,64,8,512]{4,1,2,3,0:T(8,128)(2,1)} copy(bf16[1,16,64,8,512]{4,1,3,2,0:T(8,128)(2,1)} %bitcast.13) | data formatting | bytes 16777216 | tf_op jit(solution)/shard_map/all_to_all | solution.py:131
  220.5 8.3 %fusion.12 = f32[4,1024,1,512]{3,1,0,2:T(8,128)S(1)} fusion(bf16[4,1024,1024]{2,1,0:T(8,128)(2,1)} %bitcast_select_fusion, bf16[1,1024,8,512]{3,1,2,0:T(8,128)(2,1)} %bitcast.213), kind=kOutput, calls=%fused_computation.156 | convolution fusion | flops 4294967296 | bytes 20971520 | tf_op jit(solution)/shard_map/cba,hacs->cbhs/dot_general | solution.py:135
  228.8 9.0 %fusion.13 = f32[4,1024,1,512]{3,1,0,2:T(8,128)} fusion(bf16[4,1024,1024]{2,1,0:T(8,128)(2,1)S(1)} %bitcast.212, bf16[1,1024,8,512]{3,1,2,0:T(8,128)(2,1)} %bitcast.214), kind=kOutput, calls=%fused_computation.157 | convolution fusion | flops 4294967296 | bytes 20971520 | tf_op jit(solution)/shard_map/cba,hacs->cbhs/dot_general | solution.py:141
  237.8 4.3 fusion.15
  242.0 0.6 constant_dynamic-update-slice_fusion.63
  242.7 0.6 constant_dynamic-update-slice_fusion.62
  243.3 0.6 constant_dynamic-update-slice_fusion.61
  243.9 0.6 constant_dynamic-update-slice_fusion.60
  244.6 0.6 constant_dynamic-update-slice_fusion.59
  245.2 0.6 constant_dynamic-update-slice_fusion.58
  245.8 0.6 constant_dynamic-update-slice_fusion.57
  246.5 0.6 constant_dynamic-update-slice_fusion.56
  247.1 0.6 constant_dynamic-update-slice_fusion.55
  247.7 0.6 constant_dynamic-update-slice_fusion.54
  248.4 0.6 constant_dynamic-update-slice_fusion.53
  249.0 0.6 constant_dynamic-update-slice_fusion.52
  249.6 0.6 constant_dynamic-update-slice_fusion.51
  251.6 0.6 constant_dynamic-update-slice_fusion.48
  252.8 0.6 constant_dynamic-update-slice_fusion.46
  254.1 0.6 constant_dynamic-update-slice_fusion.44
  255.4 0.6 constant_dynamic-update-slice_fusion.42
  263.6 0.6 constant_dynamic-update-slice_fusion.29
  264.9 0.6 constant_dynamic-update-slice_fusion.27
  266.1 0.6 constant_dynamic-update-slice_fusion.25
  267.4 0.6 constant_dynamic-update-slice_fusion.23
  275.7 0.6 constant_dynamic-update-slice_fusion.10
  276.9 0.6 constant_dynamic-update-slice_fusion.8
  278.2 0.6 constant_dynamic-update-slice_fusion.6
  279.5 0.6 constant_dynamic-update-slice_fusion.4
  282.6 9.0 %all-to-all-start.1 = ((bf16[64,4,2,8,512]{4,3,1,2,0:T(8,128)(2,1)}), bf16[64,4,2,8,512]{4,3,1,2,0:T(8,128)(2,1)}, u32[]{:S(2)}, u32[]{:S(2)}) async-start(bf16[64,4,2,8,512]{4,3,1,2,0:T(8,128)(2,1)} %constant_dynamic-update-slice_fusion), calls=%async_computation.1 | async-start | bytes 8388608 | tf_op jit(solution)/shard_map/all_to_all | solution.py:154
  291.7 1.0 fusion.112
  292.7 1.1 multiply_convert_fusion
  293.8 52.8 %all-to-all-done.1 = bf16[64,4,2,8,512]{4,3,1,2,0:T(8,128)(2,1)} async-done(((bf16[64,4,2,8,512]{4,3,1,2,0:T(8,128)(2,1)}), bf16[64,4,2,8,512]{4,3,1,2,0:T(8,128)(2,1)}, u32[]{:S(2)}, u32[]{:S(2)}) %all-to-all-start.1) | async-done | bytes 4194336 | tf_op jit(solution)/shard_map/all_to_all | solution.py:154
  346.6 2.7 copy.34
  349.6 1.5 collective-permute-start.1
  351.2 7.4 %fusion.18 = (f32[256,8,256]{2,0,1:T(8,128)S(1)}, f32[256,8,256]{2,0,1:T(8,128)S(1)}) fusion(f32[256]{0:T(256)S(1)} %get-tuple-element.26, f32[256]{0:T(256)S(1)} %get-tuple-element.25, f32[256,8]{0,1:T(8,128)S(1)} %broadcast_multiply_fusion), kind=kLoop, calls=%fused_computation.163 | loop fusion | flops 1048576 | bytes 4204544 | tf_op jit(solution)/shard_map/cos | solution.py:65
  358.6 19.0 %collective-permute-done.1 = bf16[256,2,8,128]{3,2,1,0:T(8,128)(2,1)S(1)} collective-permute-done((bf16[256,2,8,128]{3,2,1,0:T(8,128)(2,1)S(1)}, bf16[256,2,8,128]{3,2,1,0:T(8,128)(2,1)S(1)}, u32[]{:S(2)}, u32[]{:S(2)}) %collective-permute-start.1) | collective-permute-done | bytes 1048608 | tf_op jit(solution)/shard_map/ppermute | solution.py:13
  377.6 1.1 maximum_bitcast_fusion
  378.7 2.6 fusion.143
  381.4 2.7 copy_dynamic-update-slice_fusion.1
  384.1 3.4 copy_dynamic-update-slice_fusion
  387.5 8.1 %fusion.3 = f32[256,8,4,512]{3,0,2,1:T(8,128)} fusion(bf16[256,2,8,4,256]{4,0,3,2,1:T(8,128)(2,1)S(1)} %copy_dynamic-update-slice_fusion, bf16[256,256]{1,0:T(8,128)(2,1)S(1)} %fusion.112, bf16[256,256]{1,0:T(8,128)(2,1)S(1)} %get-tuple-element.24), kind=kOutput, calls=%fused_computation.141 | convolution fusion | flops 2148007936 | bytes 21233664 | tf_op jit(solution)/shard_map/cbml,lk->cbmk/dot_general | solution.py:80
  395.6 13.9 %convolution_add_fusion = f32[256,8,4,512]{3,0,2,1:T(8,128)} fusion(f32[256,8,4,512]{3,0,2,1:T(8,128)} %fusion.3, bf16[256,2,8,4,256]{4,0,3,2,1:T(8,128)(2,1)S(1)} %copy_dynamic-update-slice_fusion, bf16[256,256]{1,0:T(8,128)(2,1)S(1)} %get-tuple-element.24, bf16[256,256]{1,0:T(8,128)(2,1)S(1)} %get-tuple-element.23), kind=kOutput, calls=%fused_computation.128 | convolution fusion | flops 2152202240 | bytes 38010880 | tf_op jit(solution)/shard_map/cbml,lk->cbmk/dot_general | solution.py:82
  409.4 10.9 %fusion.1 = f32[256,8,4,256]{0,3,2,1:T(8,128)} fusion(f32[256,8,4,512]{3,0,2,1:T(8,128)} %convolution_add_fusion, f32[256,8,256]{2,0,1:T(8,128)S(1)} %get-tuple-element.22, f32[256,8,256]{2,0,1:T(8,128)S(1)} %get-tuple-element.21, bf16[256,128]{1,0:T(8,128)(2,1)S(1)} %get-tuple-element.12, bf16[256,128]{1,0:T(8,128)(2,1)S(1)} %slice.163), kind=kOutput, calls=%fused_computation.137 | convolution fusion | flops 1082392576 | bytes 29491200 | tf_op jit(solution)/shard_map/cbmk,kn->cbmn/dot_general | solution.py:90
  420.3 13.5 %fusion.14 = f32[256,8,4,256]{0,3,2,1:T(8,128)} fusion(f32[256,8,4,256]{0,3,2,1:T(8,128)} %fusion.1, f32[256,8,4,512]{3,0,2,1:T(8,128)} %convolution_add_fusion, f32[256,8,256]{2,0,1:T(8,128)S(1)} %get-tuple-element.22, f32[256,8,256]{2,0,1:T(8,128)S(1)} %get-tuple-element.21, bf16[256,128]{1,0:T(8,128)(2,1)S(1)} %slice.163, ...), kind=kOutput, calls=%fused_computation.158 | convolution fusion | flops 1084489728 | bytes 37879808 | tf_op jit(solution)/shard_map/cbmk,kn->cbmn/dot_general | solution.py:92
  433.8 7.7 %fusion.142 = (f32[256,8,4,128]{0,3,2,1:T(8,128)}, f32[256,8,4,128]{0,3,2,1:T(8,128)}) fusion(f32[256,8,4,256]{0,3,2,1:T(8,128)} %fusion.14), kind=kLoop, calls=%fused_computation.389 | loop fusion | bytes 16777216 | tf_op jit(solution)/shard_map/slice | solution.py:93
  441.5 5.6 %copy.39 = f32[256,1,8,512]{3,2,1,0:T(8,128)} copy(f32[256,1,8,512]{0,3,2,1:T(8,128)} %bitcast.210) | data formatting | bytes 8388608 | tf_op jit(solution)/shard_map/stack;reshape | solution.py:95
  447.1 5.5 %copy.40 = f32[256,1,8,512]{3,2,1,0:T(8,128)} copy(f32[256,1,8,512]{0,3,2,1:T(8,128)} %bitcast.209) | data formatting | bytes 8388608 | tf_op jit(solution)/shard_map/stack;reshape | solution.py:95
  452.6 8.1 %pad_maximum_fusion.1 = f32[256,2,8,512]{3,2,1,0:T(8,128)} fusion(f32[256,1,8,512]{3,2,1,0:T(8,128)} %copy.40, f32[256,1,8,512]{3,2,1,0:T(8,128)} %copy.39), kind=kLoop, calls=%fused_computation.130 | loop fusion | flops 2097152 | bytes 16777216 | tf_op jit(solution)/shard_map/stack | solution.py:95
  (59 shorter events, 25.1 us)
Async XLA Ops:
  0.9 8.3 %collective-permute-start = (bf16[16,3584]{1,0:T(8,128)(2,1)S(1)}, bf16[16,3584]{1,0:T(8,128)(2,1)S(1)}, u32[]{:S(2)}, u32[]{:S(2)}) collective-permute-start(bf16[16,3584]{1,0:T(8,128)(2,1)S(1)} %slice.107), channel_id=1, source_target_pairs={{0,64},{1,65},{2,66},{3,67},{4,68},{5,69},{6,70},{7,71},{8,72},{9,... | collective-permute-start | bytes 344072 | tf_op jit(solution)/shard_map/ppermute | solution.py:13
  84.8 127.4 %all-to-all-start = ((bf16[1,16,512,512]{3,1,0,2:T(8,128)(2,1)}), bf16[1,16,512,512]{3,1,0,2:T(8,128)(2,1)}, u32[]{:S(2)}, u32[]{:S(2)}) async-start(bf16[1,16,512,512]{3,1,0,2:T(8,128)(2,1)} %copy.32), calls=%async_computation | async-start | bytes 16777216 | tf_op jit(solution)/shard_map/all_to_all | solution.py:131
  94.6 14.8 %copy-start = (s32[1024]{0:T(1024)S(1)}, s32[1024]{0:T(1024)}, u32[]{:S(2)}) copy-start(s32[1024]{0:T(1024)} %param.8) | copy-start | bytes 12292
  212.1 16.6 %slice-start = ((s8[8388608]{0:T(1024)(128)(4,1)}), s8[4194304]{0:T(1024)(128)(4,1)S(1)}, s32[]{:S(2)}) async-start(s8[8388608]{0:T(1024)(128)(4,1)} %bitcast.211), calls=%async_computation.2 | async-start | bytes 8388608
  220.5 8.3 %slice-start.1 = ((s8[8388608]{0:T(1024)(128)(4,1)}), s8[4194304]{0:T(1024)(128)(4,1)S(1)}, s32[]{:S(2)}) async-start(s8[8388608]{0:T(1024)(128)(4,1)} %bitcast.211), calls=%async_computation.3 | async-start | bytes 8388608
  282.6 64.0 %all-to-all-start.1 = ((bf16[64,4,2,8,512]{4,3,1,2,0:T(8,128)(2,1)}), bf16[64,4,2,8,512]{4,3,1,2,0:T(8,128)(2,1)}, u32[]{:S(2)}, u32[]{:S(2)}) async-start(bf16[64,4,2,8,512]{4,3,1,2,0:T(8,128)(2,1)} %constant_dynamic-update-slice_fusion), calls=%async_computation.1 | async-start | bytes 8388608 | tf_op jit(solution)/shard_map/all_to_all | solution.py:154
  293.8 57.3 %copy-start.1 = (s32[8]{0:T(128)S(1)}, s32[8]{0:T(128)}, u32[]{:S(2)}) copy-start(s32[8]{0:T(128)} %param.9) | copy-start | bytes 100
  349.6 28.0 %collective-permute-start.1 = (bf16[256,2,8,128]{3,2,1,0:T(8,128)(2,1)S(1)}, bf16[256,2,8,128]{3,2,1,0:T(8,128)(2,1)S(1)}, u32[]{:S(2)}, u32[]{:S(2)}) collective-permute-start(bf16[256,2,8,128]{3,2,1,0:T(8,128)(2,1)S(1)} %slice.156), channel_id=1, source_target_pairs={{0,64},{1,65},{2,66},{3,67},{4,68},{5,69},{6,70},{7,71},{8,72},{9,... | collective-permute-start | bytes 3145736 | tf_op jit(solution)/shard_map/ppermute | solution.py:13
